TPU v7x, 256 devices: a whole 4x4x8 slice. The times are simulated.
256 devices in a mesh: dp: 8 (over x_lo, y), mp: 32 (over z, x_hi, core).
Axes of the slice: x: 4 (x_hi: 2, x_lo: 2; x = x_hi * 2 + x_lo), y: 4, z: 8, core: 2. Of those that a mesh axis runs over, the one named last changes fastest.
Arguments:
- tokens: bfloat16 [1024, 6144], P(('dp', 'mp')), may hold values from -6 to 6
- norm_gain: float32 [6144], replicated, may hold values from 0.5 to 1.5
- w_query: bfloat16 [6144, 4096], P('dp', 'mp'), as said below
- w_key: bfloat16 [6144, 4096], P('dp', 'mp'), as said below
- w_value: bfloat16 [6144, 4096], P('dp', 'mp'), may hold values from -0.078125 to 0.078125
- w_inner: bfloat16 [6144, 24576], P('dp', 'mp'), may hold values from -0.078125 to 0.078125
- bias_inner: float32 [24576], P('mp'), may hold values from -3 to 3
- w_attn_out: bfloat16 [4096, 6144], P('mp', 'dp'), may hold values from -0.09375 to 0.09375
- w_outer: bfloat16 [24576, 6144], P('mp', 'dp'), may hold values from -0.0390625 to 0.0390625
- temper: float32 [32], P('mp'), may hold values from 0.5 to 24
Outputs:
- result: bfloat16 [1024, 6144], P(('dp', 'mp'))
Inputs may be any that keep to these rules, and one draw needn't show every extreme that they name: `w_query`: entries of order 6144 ** -0.5. `w_key`: entries of order 6144 ** -0.5.
All inputs are finite; a program needn't handle non-finite values.
Results may differ from a plain program's by a relative error of at most 0.023.
Values may be sent and summed in bfloat16 or wider, within the bound.
No kernel may reach another device: no remote copies, remote signals or barrier semaphores. Data moves between devices by JAX's collectives and lax.ppermute only.
A program may use at most 64 MiB of HBM per device.

v0:
```python
import functools
import math

import jax
import jax.numpy as jnp
from jax import lax
from jax.experimental import pallas as pl
from jax.experimental.pallas import tpu as pltpu
from jax.sharding import Mesh
from jax.sharding import PartitionSpec as P


HEAD = 128
DP = ("xl", "y")
MP = ("z", "xh", "c")
ALL = DP + MP
BF = jnp.bfloat16
F32 = jnp.float32
ANY = pl.BlockSpec(memory_space=pl.ANY)
VMEM = pl.BlockSpec(memory_space=pltpu.VMEM)


def normalize(values):
    center = values - jnp.mean(values, axis=-1, keepdims=True)
    spread = jnp.mean(center * center, axis=-1, keepdims=True)
    return center * lax.rsqrt(spread + 1e-06)


def partner(array, axis):
    return lax.ppermute(array, axis, [(0, 1), (1, 0)])


def exchange(pieces, axes):
    return lax.all_to_all(pieces, axes, split_axis=0, concat_axis=0, tiled=True)


def dot(a, b):
    return lax.dot_general(a, b, (((a.ndim - 1,), (0,)), ((), ())), preferred_element_type=F32)


def params(mib):
    return pltpu.CompilerParams(vmem_limit_bytes=mib * 1024 * 1024)


def cost(flops, moved):
    return pl.CostEstimate(flops=flops, bytes_accessed=moved, transcendentals=0)


def norm_kernel(tokens, norm_gain, normed, gain, own, sems):
    copies = [
        pltpu.make_async_copy(tokens, own, sems.at[0]),
        pltpu.make_async_copy(norm_gain, gain, sems.at[1]),
    ]
    for copy in copies:
        copy.start()
    copies[0].wait()
    values = normalize(own[...].astype(F32))
    copies[1].wait()
    normed[...] = values * gain[...]


def norm_own(tokens, gain):
    count, width = tokens.shape
    return pl.pallas_call(
        norm_kernel,
        out_shape=(
            jax.ShapeDtypeStruct((count, width), F32),
            jax.ShapeDtypeStruct((1, width), F32),
        ),
        in_specs=[ANY] * 2,
        out_specs=(VMEM, VMEM),
        scratch_shapes=[pltpu.VMEM((count, width), BF), pltpu.SemaphoreType.DMA((2,))],
        compiler_params=params(8),
        cost_estimate=cost(100 * count * width, 1024 * 1024),
        name="norm_own",
    )(tokens, gain.reshape(1, width))


def spread_kernel(n_y, n_z, normed_own, gain, beside, out):
    _, width = beside.shape
    cols = width // (2 * n_y)
    mine = normed_own[...]
    theirs = normalize(beside[...].astype(F32)) * gain[...]
    first = lax.axis_index("xh") == 0
    normed = jnp.concatenate(
        (jnp.where(first, mine, theirs), jnp.where(first, theirs, mine)), axis=0
    )
    lower = lax.axis_index("xl") == 0
    for y in range(n_y):
        a = normed[:, y * cols : (y + 1) * cols]
        b = normed[:, (n_y + y) * cols : (n_y + y + 1) * cols]
        left = jnp.where(lower, a, b).astype(BF)
        right = jnp.where(lower, b, a).astype(BF)
        for z in range(n_z):
            out[z * n_y + y, :, :cols] = left
            out[z * n_y + y, :, cols:] = right


def spread(normed_own, gain, beside, n_y, n_z):
    count, width = beside.shape
    return pl.pallas_call(
        functools.partial(spread_kernel, n_y, n_z),
        out_shape=jax.ShapeDtypeStruct((n_z * n_y, 2 * count, width // n_y), BF),
        in_specs=[VMEM] * 3,
        out_specs=VMEM,
        compiler_params=params(8),
        cost_estimate=cost(20 * count * width, 2 * 1024 * 1024),
        name="normed_pieces",
    )(normed_own, gain, beside)


def product(rows, w, w_p, at):
    cols = rows.shape[1] // 2
    return dot(rows[:, :cols], w[:, at]) + dot(rows[:, cols:], w_p[:, at])


def store(out, value, first, at):
    n_y = out.shape[0]
    value = value.astype(BF).reshape(-1, n_y, 8, value.shape[-1])
    for y in range(n_y):
        part = value[:, y].reshape(-1, value.shape[-1])
        out[y, first : first + part.shape[0], at] = part


def inner_kernel(tokens, w_own, w_other, out, rows, kept, kept_p, sems):
    chunk = 384
    first = pltpu.make_async_copy(tokens, rows, sems.at[0])
    copies = []
    for n in range(kept.shape[1] // chunk):
        at = pl.ds(n * chunk, chunk)
        for m, (source, to) in enumerate(((w_own, kept), (w_other, kept_p))):
            copies.append(
                pltpu.make_async_copy(source.at[:, at], to.at[:, at], sems.at[1 + 2 * n + m])
            )
    copies[0].start()
    first.start()
    for copy in copies[1:]:
        copy.start()
    first.wait()
    left = rows[...].reshape(-1, rows.shape[-1])
    for n in range(kept.shape[1] // chunk):
        copies[2 * n].wait()
        copies[2 * n + 1].wait()
        at = slice(n * chunk, (n + 1) * chunk)
        store(out, product(left, kept, kept_p, at), 0, at)


def inner_part(tokens, w_own, w_other, images):
    pieces, count, width = tokens.shape
    half = pieces * count // images
    columns = w_own.shape[1]
    return pl.pallas_call(
        inner_kernel,
        out_shape=jax.ShapeDtypeStruct((images, half, columns), BF),
        in_specs=[ANY, ANY, ANY],
        out_specs=VMEM,
        scratch_shapes=[
            pltpu.VMEM(tokens.shape, BF),
            pltpu.VMEM(w_own.shape, BF),
            pltpu.VMEM(w_other.shape, BF),
            pltpu.SemaphoreType.DMA((5,)),
        ],
        compiler_params=params(12),
        cost_estimate=cost(2 * images * half * width * columns, 4 * 1024 * 1024),
        name="inner_part",
    )(tokens, w_own, w_other)


def heads_kernel(
    mine, theirs, w_own, w_other, inner_mine, inner_theirs, out, rows, rows_p, kept, kept_p, sems
):
    width, wide = rows.shape[-1], w_own.shape[1]
    half = out.shape[1] // 2
    copies = [
        pltpu.make_async_copy(mine, rows, sems.at[0]),
        pltpu.make_async_copy(w_own, kept, sems.at[1]),
        pltpu.make_async_copy(w_other, kept_p, sems.at[2]),
        pltpu.make_async_copy(theirs, rows_p, sems.at[3]),
        pltpu.make_async_copy(inner_mine, out.at[:, :half, wide:], sems.at[4]),
        pltpu.make_async_copy(inner_theirs, out.at[:, half:, wide:], sems.at[5]),
    ]
    for copy in copies:
        copy.start()
    cols = width // 2
    copies[0].wait()
    copies[1].wait()
    left = rows[...].reshape(-1, width)
    own = dot(left[:, :cols], kept[...])
    copies[2].wait()
    store(out, own + dot(left[:, cols:], kept_p[...]), 0, slice(0, wide))
    copies[3].wait()
    left = rows_p[...].reshape(-1, width)
    value = dot(left[:, :cols], kept[...]) + dot(left[:, cols:], kept_p[...])
    store(out, value, half, slice(0, wide))
    for copy in copies[4:]:
        copy.wait()


def heads_part(mine, theirs, w_own, w_other, inner_mine, inner_theirs):
    images, half, _ = inner_mine.shape
    width, wide = mine.shape[-1], w_own.shape[1]
    return pl.pallas_call(
        heads_kernel,
        out_shape=jax.ShapeDtypeStruct((images, 2 * half, wide + inner_mine.shape[2]), BF),
        in_specs=[ANY, ANY, ANY, ANY, ANY, ANY],
        out_specs=VMEM,
        scratch_shapes=[pltpu.VMEM(mine.shape, BF)] * 2
        + [pltpu.VMEM(w_own.shape, BF)] * 2
        + [pltpu.SemaphoreType.DMA((6,))],
        compiler_params=params(12),
        cost_estimate=cost(4 * images * half * width * wide, 4 * 1024 * 1024),
        name="heads_part",
    )(mine, theirs, w_own, w_other, inner_mine, inner_theirs)


def middle_kernel(arrived, bias, scale, out, kept, sem):
    copy = pltpu.make_async_copy(bias, kept, sem)
    copy.start()
    copies, columns = out.shape[0], kept.shape[0]

    def summed(at):
        total = arrived[0, :, at].astype(F32)
        for n in range(1, arrived.shape[0]):
            total = total + arrived[n, :, at].astype(F32)
        return total

    def rounded(n):
        return summed(slice(n * HEAD, (n + 1) * HEAD)).astype(BF)

    query_norm = normalize(rounded(0).astype(F32)).astype(BF)
    key_norm = normalize(rounded(1).astype(F32)).astype(BF)
    scores = lax.dot_general(
        query_norm, key_norm, (((1,), (1,)), ((), ())), preferred_element_type=F32
    )
    scores = scores * scale[0]
    powers = jnp.exp(scores - jnp.max(scores, axis=-1, keepdims=True))
    probs = (powers / jnp.sum(powers, axis=-1, keepdims=True)).astype(BF)
    mixed = dot(probs, rounded(2)).astype(BF)
    for n in range(copies):
        out[n, :, :HEAD] = mixed
    copy.wait()
    for m in range(columns // 256):
        at = slice(m * 256, (m + 1) * 256)
        inner = summed(slice(3 * HEAD + m * 256, 3 * HEAD + (m + 1) * 256)) + kept[at]
        activ = (inner * (0.5 + 0.5 * lax.erf(inner * math.sqrt(0.5)))).astype(BF)
        for n in range(copies):
            out[n, :, HEAD + m * 256 : HEAD + (m + 1) * 256] = activ


def middle(arrived, bias, scale):
    _, patches, _ = arrived.shape
    columns = bias.shape[0]
    return pl.pallas_call(
        middle_kernel,
        out_shape=jax.ShapeDtypeStruct((1, patches, HEAD + columns), BF),
        in_specs=[VMEM, ANY, pl.BlockSpec(memory_space=pltpu.SMEM)],
        out_specs=VMEM,
        scratch_shapes=[pltpu.VMEM((columns,), F32), pltpu.SemaphoreType.DMA],
        compiler_params=params(12),
        cost_estimate=cost(60 * patches * columns, 2 * 1024 * 1024),
        name="middle",
    )(arrived, bias, scale)


def output_kernel(part, features, w_own, w_other, out, rows, kept_own, kept_other, sems):
    images, half, width = rows.shape
    cols = kept_own.shape[1]
    copies = [
        pltpu.make_async_copy(
            features.at[:, part * half : (part + 1) * half], rows, sems.at[0]
        ),
        pltpu.make_async_copy(w_own, kept_own, sems.at[1]),
        pltpu.make_async_copy(w_other, kept_other, sems.at[2]),
    ]
    for copy in copies:
        copy.start()
    copies[0].wait()
    left = rows[...].reshape(images * half, width)
    for n, kept in enumerate((kept_own, kept_other)):
        copies[n + 1].wait()
        for m in range(2):
            at = slice(m * cols // 2, (m + 1) * cols // 2)
            value = dot(left, kept[:, at]).astype(out.dtype).reshape(images, half, cols // 2)
            out[:, :, n * cols + m * cols // 2 : n * cols + (m + 1) * cols // 2] = value


def output(features, w_own, w_other, part, kind):
    images, patches, width = features.shape
    half, cols = patches // 2, w_own.shape[1]
    return pl.pallas_call(
        functools.partial(output_kernel, part),
        out_shape=jax.ShapeDtypeStruct((images, half, 2 * cols), kind),
        in_specs=[ANY] * 3,
        out_specs=VMEM,
        scratch_shapes=[
            pltpu.VMEM((images, half, width), BF),
            pltpu.VMEM(w_own.shape, BF),
            pltpu.VMEM(w_other.shape, BF),
            pltpu.SemaphoreType.DMA((3,)),
        ],
        compiler_params=params(16),
        cost_estimate=cost(4 * images * half * width * cols, 4 * 1024 * 1024),
        name="output_sent" if part else "output_kept",
    )(features, w_own, w_other)


def combine_kernel(n_xh, kept, received, out):
    images, half, _ = kept.shape
    n_z = half // 8
    count = 8 // n_xh
    for y in range(images):
        for z in range(n_z):
            at = slice(z * 8, (z + 1) * 8)
            value = kept[y, at] + received[y, at].astype(F32)
            for xh in range(n_xh):
                out[(xh * n_z + z) * images + y] = value[xh * count : (xh + 1) * count].astype(BF)


def combine(kept, received, n_xh):
    images, half, width = kept.shape
    count = 8 // n_xh
    return pl.pallas_call(
        functools.partial(combine_kernel, n_xh),
        out_shape=jax.ShapeDtypeStruct((images * half // count, count, width), BF),
        in_specs=[VMEM] * 2,
        out_specs=VMEM,
        compiler_params=params(8),
        cost_estimate=cost(kept.size, 4 * 1024 * 1024),
        name="combine",
    )(kept, received)


def finish_kernel(n_y, arrived, tokens, out):
    pieces, _, width = arrived.shape
    cols = width // 2
    lower = lax.axis_index("xl") == 0
    for y in range(n_y):
        total = arrived[y].astype(F32)
        for n in range(y + n_y, pieces, n_y):
            total = total + arrived[n].astype(F32)
        left, right = total[:, :cols], total[:, cols:]
        for n, value in enumerate(
            (jnp.where(lower, left, right), jnp.where(lower, right, left))
        ):
            to = slice((n * n_y + y) * cols, (n * n_y + y + 1) * cols)
            out[:, to] = (tokens[:, to].astype(F32) + value).astype(BF)


def finish(arrived, tokens, n_y):
    return pl.pallas_call(
        functools.partial(finish_kernel, n_y),
        out_shape=jax.ShapeDtypeStruct(tokens.shape, BF),
        in_specs=[VMEM] * 2,
        out_specs=VMEM,
        compiler_params=params(8),
        cost_estimate=cost(arrived.size, 2 * 1024 * 1024),
        name="finish",
    )(arrived, tokens)


def block(
    tokens, norm_gain, w_query, w_key, w_value, w_inner, bias_inner, w_attn_out, w_outer, temper
):
    n_y, n_z, n_xh = (lax.axis_size(a) for a in ("y", "z", "xh"))
    beside = partner(tokens, "xh")
    w_qkv = jnp.concatenate((w_query, w_key, w_value), axis=1)
    w_inner_p = partner(w_inner, "xl")
    w_qkv_p = partner(w_qkv, "xl")
    w_out = jnp.concatenate((w_attn_out, w_outer), axis=0)
    w_out_p = partner(w_out, "xl")
    normed, gain = norm_own(tokens, norm_gain)
    pieces = spread(normed, gain, beside, n_y, n_z)
    mine = exchange(pieces, ("z", "y"))
    theirs = partner(mine, "c")
    inner_mine = inner_part(mine, w_inner, w_inner_p, n_y)
    inner_theirs = inner_part(theirs, w_inner, w_inner_p, n_y)
    partial = heads_part(mine, theirs, w_qkv, w_qkv_p, inner_mine, inner_theirs)
    arrived = exchange(partial, "y")
    scale = temper / math.sqrt(HEAD)
    features = middle(arrived, bias_inner, scale)[0]
    features = lax.all_gather(features, "y", axis=0, tiled=False)
    sent = partner(output(features, w_out, w_out_p, 1, BF), "c")
    kept = output(features, w_out, w_out_p, 0, F32)
    pieces = combine(kept, sent, n_xh)
    arrived = exchange(pieces, ("xh", "z", "y"))
    return finish(arrived, tokens, n_y)


def solution(mesh):
    finer = Mesh(mesh.devices.reshape(2, 4, 8, 2, 2), ALL)
    return jax.shard_map(
        block,
        mesh=finer,
        in_specs=(
            P(ALL, None),
            P(),
            P(DP, MP),
            P(DP, MP),
            P(DP, MP),
            P(DP, MP),
            P(MP),
            P(MP, DP),
            P(MP, DP),
            P(MP),
        ),
        out_specs=P(ALL, None),
        check_vma=False,
    )
```

profile of v0, /device:TPU:8, one launch (start us, length us, event | category | flops | bytes accessed | tf_op | source)
XLA Modules:
  0.0 135.1 jit_solution(1166940564773661253)
XLA Ops:
  0.0 3.0 %collective-permute-start = (bf16[4,6144]{1,0:T(4,128)(2,1)}, bf16[4,6144]{1,0:T(4,128)(2,1)S(1)}, u32[]{:S(2)}, u32[]{:S(2)}) collective-permute-start(bf16[4,6144]{1,0:T(4,128)(2,1)} %tokens.3), channel_id=1, source_target_pairs={{0,2},{2,0},{1,3},{3,1},{4,6},{6,4},{5,7},{7,5},{8,10},{10,8},{9,1... | collective-permute-start | bytes 147464 | tf_op jit(solution)/shard_map/ppermute | solution.py:30
  3.0 0.0 copy-start.1
  3.0 0.8 copy-done.1
  3.9 0.0 copy-start.3
  3.9 0.7 copy-done.3
  4.6 0.0 copy-start.6
  4.6 0.4 norm_own.1
  5.0 0.8 collective-permute-done.beside
  5.8 0.0 copy-start.7
  5.8 1.2 normed_pieces.1
  7.0 0.0 copy-start.8
  7.0 0.0 copy-start.5
  7.0 11.8 %all-to-all-start = ((bf16[32,8,1536]{2,1,0:T(8,128)(2,1)}), bf16[32,8,1536]{2,1,0:T(8,128)(2,1)S(1)}, u32[]{:S(2)}, u32[]{:S(2)}) async-start(bf16[32,8,1536]{2,1,0:T(8,128)(2,1)} %normed_pieces.1), calls=%async_computation | async-start | bytes 1572864 | tf_op jit(solution)/shard_map/all_to_all | solution.py:34
  18.9 1.6 %collective-permute-start.3 = (bf16[768,768]{1,0:T(8,128)(2,1)}, bf16[768,768]{1,0:T(8,128)(2,1)}, u32[]{:S(2)}, u32[]{:S(2)}) collective-permute-start(bf16[768,768]{1,0:T(8,128)(2,1)} %w_own.3), channel_id=1, source_target_pairs={{0,128},{128,0},{1,129},{129,1},{2,130},{130,2},{3,131},{131,3},{4... | collective-permute-start | bytes 3538952 | tf_op jit(solution)/shard_map/ppermute | solution.py:30
  20.5 19.8 %all-to-all-done.tokens.mine = bf16[32,8,1536]{2,1,0:T(8,128)(2,1)S(1)} async-done(((bf16[32,8,1536]{2,1,0:T(8,128)(2,1)}), bf16[32,8,1536]{2,1,0:T(8,128)(2,1)S(1)}, u32[]{:S(2)}, u32[]{:S(2)}) %all-to-all-start) | async-done | bytes 786464 | tf_op jit(solution)/shard_map/all_to_all | solution.py:34
  40.2 0.0 collective-permute-start.1
  40.2 0.0 copy-done.6
  40.3 0.0 copy-done.7
  40.4 0.0 copy-done.8
  40.4 1.5 %collective-permute-start.2 = (bf16[768,384]{1,0:T(8,128)(2,1)S(1)}, bf16[768,384]{1,0:T(8,128)(2,1)S(1)}, u32[]{:S(2)}, u32[]{:S(2)}) collective-permute-start(bf16[768,384]{1,0:T(8,128)(2,1)S(1)} %constant_dynamic-update-slice_fusion.w_own), channel_id=1, source_target_pairs={{0,128},{128,0},{1,129},{129,1},{2,130},{130,2},{3,131},{131,3},{4... | collective-permute-start | bytes 1769480 | tf_op jit(solution)/shard_map/ppermute | solution.py:30
  41.9 0.9 constant_dynamic-update-slice_fusion.4
  42.9 0.0 copy-done.5
  42.9 0.1 constant_dynamic-update-slice_fusion.3.w_own
  43.0 0.7 collective-permute-start.4
  43.7 3.3 %collective-permute-done.3.w_other = bf16[768,768]{1,0:T(8,128)(2,1)} collective-permute-done((bf16[768,768]{1,0:T(8,128)(2,1)}, bf16[768,768]{1,0:T(8,128)(2,1)}, u32[]{:S(2)}, u32[]{:S(2)}) %collective-permute-start.3) | collective-permute-done | bytes 1179680 | tf_op jit(solution)/shard_map/ppermute | solution.py:30
  47.0 2.5 %inner_part.2.inner_mine = bf16[4,64,768]{2,1,0:T(8,128)(2,1)S(1)} custom-call(bf16[32,8,1536]{2,1,0:T(8,128)(2,1)S(1)} %all-to-all-done.tokens.mine, bf16[768,768]{1,0:T(8,128)(2,1)} %w_own.3, bf16[768,768]{1,0:T(8,128)(2,1)} %collective-permute-done.3.w_other), custom_call_target="tpu_custom_call" | custom-call | flops 603979776 | bytes 4194304 | tf_op jit(solution)/shard_map/inner_part/pallas_call | solution.py:152
  49.4 0.0 collective-permute-done.1.tokens.theirs
  49.5 2.5 %inner_part.3.inner_theirs = bf16[4,64,768]{2,1,0:T(8,128)(2,1)S(1)} custom-call(bf16[32,8,1536]{2,1,0:T(8,128)(2,1)S(1)} %collective-permute-done.1.tokens.theirs, bf16[768,768]{1,0:T(8,128)(2,1)} %w_own.3, bf16[768,768]{1,0:T(8,128)(2,1)} %collective-permute-done.3.w_other), custom_call_target="tpu_custom_call" | custom-call | flops 603979776 | bytes 4194304 | tf_op jit(solution)/shard_map/inner_part/pallas_call | solution.py:152
  51.9 7.6 %collective-permute-done.2.w_other = bf16[768,384]{1,0:T(8,128)(2,1)S(1)} collective-permute-done((bf16[768,384]{1,0:T(8,128)(2,1)S(1)}, bf16[768,384]{1,0:T(8,128)(2,1)S(1)}, u32[]{:S(2)}, u32[]{:S(2)}) %collective-permute-start.2) | collective-permute-done | bytes 589856 | tf_op jit(solution)/shard_map/ppermute | solution.py:30
  59.5 1.7 %heads_part.1 = bf16[4,128,1152]{2,1,0:T(8,128)(2,1)S(1)} custom-call(bf16[32,8,1536]{2,1,0:T(8,128)(2,1)S(1)} %all-to-all-done.tokens.mine, bf16[32,8,1536]{2,1,0:T(8,128)(2,1)S(1)} %collective-permute-done.1.tokens.theirs, bf16[768,384]{1,0:T(8,128)(2,1)S(1)} %constant_dynamic-update-slice_fusion.w_own, ...), custom_call_target="tpu_custom_call" | custom-call | flops 603979776 | bytes 4194304 | tf_op jit(solution)/shard_map/heads_part/pallas_call | solution.py:202
  61.2 0.0 copy-start
  61.2 1.0 copy-done
  62.2 0.0 copy-start.4
  62.2 4.9 %all-to-all-start.1 = ((bf16[4,128,1152]{2,1,0:T(8,128)(2,1)}), bf16[4,128,1152]{2,1,0:T(8,128)(2,1)}, u32[]{:S(2)}, u32[]{:S(2)}) async-start(bf16[4,128,1152]{2,1,0:T(8,128)(2,1)} %copy-done), calls=%async_computation.1 | async-start | bytes 2359296 | tf_op jit(solution)/shard_map/all_to_all | solution.py:34
  67.8 12.0 %all-to-all-done.1.arrived = bf16[4,128,1152]{2,1,0:T(8,128)(2,1)} async-done(((bf16[4,128,1152]{2,1,0:T(8,128)(2,1)}), bf16[4,128,1152]{2,1,0:T(8,128)(2,1)}, u32[]{:S(2)}, u32[]{:S(2)}) %all-to-all-start.1) | async-done | bytes 1179680 | tf_op jit(solution)/shard_map/all_to_all | solution.py:34
  79.8 0.0 copy-done.4
  79.8 2.1 %middle.1 = bf16[1,128,896]{2,1,0:T(8,128)(2,1)S(1)} custom-call(bf16[4,128,1152]{2,1,0:T(8,128)(2,1)} %all-to-all-done.1.arrived, f32[768]{0:T(1024)S(1)} %copy-done.4, f32[1]{0:T(128)S(6)} %div.3.scale), custom_call_target="tpu_custom_call" | custom-call | flops 5898240 | bytes 2097152 | tf_op jit(solution)/shard_map/middle/pallas_call | solution.py:253
  81.9 14.1 %all_gather.3.features = bf16[4,128,896]{2,1,0:T(8,128)(2,1)S(1)} all-gather(bf16[1,128,896]{2,1,0:T(8,128)(2,1)S(1)} %middle.1), channel_id=1, replica_groups=mesh['xl'=2,'y'=4,'z'=8,'xh'=2,'c'=2] {'y'}, dimensions={0}, use_global_device_ids=true | all-gather | bytes 1146880 | tf_op jit(solution)/shard_map/all_gather | solution.py:381
  96.0 0.0 collective-permute-done.4.w_other
  96.0 1.8 %output_sent.1 = bf16[4,64,1536]{2,1,0:T(8,128)(2,1)S(1)} custom-call(bf16[4,128,896]{2,1,0:T(8,128)(2,1)S(1)} %all_gather.3.features, bf16[896,768]{1,0:T(8,128)(2,1)S(1)} %constant_dynamic-update-slice_fusion.3.w_own, bf16[896,768]{1,0:T(8,128)(2,1)S(1)} %collective-permute-done.4.w_other), custom_call_target="tpu_custom_call" | custom-call | flops 704643072 | bytes 4194304 | tf_op jit(solution)/shard_map/output_sent/pallas_call | solution.py:290
  97.9 0.1 collective-permute-start.5
  98.0 1.8 %output_kept.1.kept = f32[4,64,1536]{2,1,0:T(8,128)S(1)} custom-call(bf16[4,128,896]{2,1,0:T(8,128)(2,1)S(1)} %all_gather.3.features, bf16[896,768]{1,0:T(8,128)(2,1)S(1)} %constant_dynamic-update-slice_fusion.3.w_own, bf16[896,768]{1,0:T(8,128)(2,1)S(1)} %collective-permute-done.4.w_other), custom_call_target="tpu_custom_call" | custom-call | flops 704643072 | bytes 4194304 | tf_op jit(solution)/shard_map/output_kept/pallas_call | solution.py:290
  99.8 0.4 collective-permute-done.5.received
  100.2 0.2 combine.1
  100.4 0.0 copy-start.2
  100.4 34.0 %all_to_all.15.arrived = bf16[64,4,1536]{2,1,0:T(4,128)(2,1)S(1)} all-to-all(bf16[64,4,1536]{2,1,0:T(4,128)(2,1)S(1)} %combine.1), channel_id=1, replica_groups=mesh['xl'=2,'y'=4,'z'=8,'xh'=2,'c'=2] {'xh','z','y'}, dimensions={0} | all-to-all | bytes 1572864 | tf_op jit(solution)/shard_map/all_to_all | solution.py:34
  134.4 0.0 copy-done.2
  134.4 0.7 finish.1
  (3 shorter events, 0.1 us)
Async XLA Ops:
  0.0 5.8 %collective-permute-start = (bf16[4,6144]{1,0:T(4,128)(2,1)}, bf16[4,6144]{1,0:T(4,128)(2,1)S(1)}, u32[]{:S(2)}, u32[]{:S(2)}) collective-permute-start(bf16[4,6144]{1,0:T(4,128)(2,1)} %tokens.3), channel_id=1, source_target_pairs={{0,2},{2,0},{1,3},{3,1},{4,6},{6,4},{5,7},{7,5},{8,10},{10,8},{9,1... | collective-permute-start | bytes 147464 | tf_op jit(solution)/shard_map/ppermute | solution.py:30
  3.0 0.8 copy-start.1
  3.9 0.7 copy-start.3
  4.6 35.7 %copy-start.6 = (bf16[768,128]{1,0:T(8,128)(2,1)S(1)}, bf16[768,128]{1,0:T(8,128)(2,1)}, u32[]{:S(2)}) copy-start(bf16[768,128]{1,0:T(8,128)(2,1)} %param.12) | copy-start | bytes 589828
  5.8 34.5 %copy-start.7 = (bf16[768,128]{1,0:T(8,128)(2,1)S(1)}, bf16[768,128]{1,0:T(8,128)(2,1)}, u32[]{:S(2)}) copy-start(bf16[768,128]{1,0:T(8,128)(2,1)} %param.13) | copy-start | bytes 589828
  7.0 33.3 %copy-start.8 = (bf16[768,128]{1,0:T(8,128)(2,1)S(1)}, bf16[768,128]{1,0:T(8,128)(2,1)}, u32[]{:S(2)}) copy-start(bf16[768,128]{1,0:T(8,128)(2,1)} %param.14) | copy-start | bytes 589828
  7.0 35.8 %copy-start.5 = (bf16[768,768]{1,0:T(8,128)(2,1)S(1)}, bf16[768,768]{1,0:T(8,128)(2,1)}, u32[]{:S(2)}) copy-start(bf16[768,768]{1,0:T(8,128)(2,1)} %param.18) | copy-start | bytes 3538948
  7.0 33.2 %all-to-all-start = ((bf16[32,8,1536]{2,1,0:T(8,128)(2,1)}), bf16[32,8,1536]{2,1,0:T(8,128)(2,1)S(1)}, u32[]{:S(2)}, u32[]{:S(2)}) async-start(bf16[32,8,1536]{2,1,0:T(8,128)(2,1)} %normed_pieces.1), calls=%async_computation | async-start | bytes 1572864 | tf_op jit(solution)/shard_map/all_to_all | solution.py:34
  18.9 28.1 %collective-permute-start.3 = (bf16[768,768]{1,0:T(8,128)(2,1)}, bf16[768,768]{1,0:T(8,128)(2,1)}, u32[]{:S(2)}, u32[]{:S(2)}) collective-permute-start(bf16[768,768]{1,0:T(8,128)(2,1)} %w_own.3), channel_id=1, source_target_pairs={{0,128},{128,0},{1,129},{129,1},{2,130},{130,2},{3,131},{131,3},{4... | collective-permute-start | bytes 3538952 | tf_op jit(solution)/shard_map/ppermute | solution.py:30
  40.2 9.2 %collective-permute-start.1 = (bf16[32,8,1536]{2,1,0:T(8,128)(2,1)S(1)}, bf16[32,8,1536]{2,1,0:T(8,128)(2,1)S(1)}, u32[]{:S(2)}, u32[]{:S(2)}) collective-permute-start(bf16[32,8,1536]{2,1,0:T(8,128)(2,1)S(1)} %all-to-all-done.tokens.mine), channel_id=1, source_target_pairs={{0,1},{1,0},{2,3},{3,2},{4,5},{5,4},{6,7},{7,6},{8,9},{9,8},{10,11... | collective-permute-start | bytes 2359304 | tf_op jit(solution)/shard_map/ppermute | solution.py:30
  40.4 19.1 %collective-permute-start.2 = (bf16[768,384]{1,0:T(8,128)(2,1)S(1)}, bf16[768,384]{1,0:T(8,128)(2,1)S(1)}, u32[]{:S(2)}, u32[]{:S(2)}) collective-permute-start(bf16[768,384]{1,0:T(8,128)(2,1)S(1)} %constant_dynamic-update-slice_fusion.w_own), channel_id=1, source_target_pairs={{0,128},{128,0},{1,129},{129,1},{2,130},{130,2},{3,131},{131,3},{4... | collective-permute-start | bytes 1769480 | tf_op jit(solution)/shard_map/ppermute | solution.py:30
  43.0 53.0 %collective-permute-start.4 = (bf16[896,768]{1,0:T(8,128)(2,1)S(1)}, bf16[896,768]{1,0:T(8,128)(2,1)S(1)}, u32[]{:S(2)}, u32[]{:S(2)}) collective-permute-start(bf16[896,768]{1,0:T(8,128)(2,1)S(1)} %constant_dynamic-update-slice_fusion.3.w_own), channel_id=1, source_target_pairs={{0,128},{128,0},{1,129},{129,1},{2,130},{130,2},{3,131},{131,3},{4... | collective-permute-start | bytes 4128776 | tf_op jit(solution)/shard_map/ppermute | solution.py:30
  61.2 1.0 copy-start
  62.2 17.5 %copy-start.4 = (f32[768]{0:T(1024)S(1)}, f32[768]{0:T(1024)}, u32[]{:S(2)}) copy-start(f32[768]{0:T(1024)} %bias.1) | copy-start | bytes 9220
  62.2 17.5 %all-to-all-start.1 = ((bf16[4,128,1152]{2,1,0:T(8,128)(2,1)}), bf16[4,128,1152]{2,1,0:T(8,128)(2,1)}, u32[]{:S(2)}, u32[]{:S(2)}) async-start(bf16[4,128,1152]{2,1,0:T(8,128)(2,1)} %copy-done), calls=%async_computation.1 | async-start | bytes 2359296 | tf_op jit(solution)/shard_map/all_to_all | solution.py:34
  97.9 2.4 %collective-permute-start.5 = (bf16[4,64,1536]{2,1,0:T(8,128)(2,1)S(1)}, bf16[4,64,1536]{2,1,0:T(8,128)(2,1)S(1)}, u32[]{:S(2)}, u32[]{:S(2)}) collective-permute-start(bf16[4,64,1536]{2,1,0:T(8,128)(2,1)S(1)} %output_sent.1), channel_id=1, source_target_pairs={{0,1},{1,0},{2,3},{3,2},{4,5},{5,4},{6,7},{7,6},{8,9},{9,8},{10,11... | collective-permute-start | bytes 2359304 | tf_op jit(solution)/shard_map/ppermute | solution.py:30
  100.4 34.0 %copy-start.2 = (bf16[4,6144]{1,0:T(4,128)(2,1)S(1)}, bf16[4,6144]{1,0:T(4,128)(2,1)}, u32[]{:S(2)}) copy-start(bf16[4,6144]{1,0:T(4,128)(2,1)} %tokens.3) | copy-start | bytes 147460
where the time goes:
time: 138 us; the launch traced here: 135 us
  blocking collectives  48.1 us (35%)
  waiting for transfers between devices  43.9 us (32%)
  starting transfers between devices  23.7 us (17%)
  Pallas kernels  15 us (11%)
  local copies, waits for them, and re-layouts  3.74 us (3%)
    all_to_all x1, blocking collectives, exchange(): return lax.all_to_all(pieces, axes, split_axis=0, concat_axis=0, tiled=True)  34 us
    all_to_all x2, waiting for transfers between devices, exchange(): return lax.all_to_all(pieces, axes, split_axis=0, concat_axis=0, tiled=True)  31.7 us
    all_to_all x2, starting transfers between devices, exchange(): return lax.all_to_all(pieces, axes, split_axis=0, concat_axis=0, tiled=True)  16.8 us
    all_gather x1, blocking collectives, block(): features = lax.all_gather(features, 'y', axis=0, tiled=False)  14.1 us
    ppermute x6, waiting for transfers between devices, partner(): return lax.ppermute(array, axis, [(0, 1), (1, 0)])  12.2 us
    ppermute x6, starting transfers between devices, partner(): return lax.ppermute(array, axis, [(0, 1), (1, 0)])  6.9 us
    pallas_call x2, Pallas kernels, inner_part(): pl.pallas_call(inner_kernel, out_shape=jax.ShapeDtypeStruct((images, half...  4.93 us
    pallas_call x2, Pallas kernels, output(): pl.pallas_call(functools.partial(output_kernel, part), out_shape=jax.Shap...  3.67 us
  transfers between devices with their start and end apart: 8, of which 6 were waited for; matrix products, arithmetic and copies ran while one was open for 1% of the time, Pallas kernels for 8%

commit v1 on v0

--- a/solution.py
+++ b/solution.py
@@ -122,27 +122,20 @@
         out[y, first : first + part.shape[0], at] = part
 
 
-def inner_kernel(tokens, w_own, w_other, out, rows, kept, kept_p, sems):
+def inner_kernel(rows, w_own, w_other, out, kept_p, sems):
     chunk = 384
-    first = pltpu.make_async_copy(tokens, rows, sems.at[0])
+    chunks = w_own.shape[1] // chunk
     copies = []
-    for n in range(kept.shape[1] // chunk):
+    for n in range(chunks):
         at = pl.ds(n * chunk, chunk)
-        for m, (source, to) in enumerate(((w_own, kept), (w_other, kept_p))):
-            copies.append(
-                pltpu.make_async_copy(source.at[:, at], to.at[:, at], sems.at[1 + 2 * n + m])
-            )
-    copies[0].start()
-    first.start()
-    for copy in copies[1:]:
+        copies.append(pltpu.make_async_copy(w_other.at[:, at], kept_p.at[:, at], sems.at[n]))
+    for copy in copies:
         copy.start()
-    first.wait()
     left = rows[...].reshape(-1, rows.shape[-1])
-    for n in range(kept.shape[1] // chunk):
-        copies[2 * n].wait()
-        copies[2 * n + 1].wait()
+    for n in range(chunks):
+        copies[n].wait()
         at = slice(n * chunk, (n + 1) * chunk)
-        store(out, product(left, kept, kept_p, at), 0, at)
+        store(out, product(left, w_own, kept_p, at), 0, at)
 
 
 def inner_part(tokens, w_own, w_other, images):
@@ -152,14 +145,9 @@
     return pl.pallas_call(
         inner_kernel,
         out_shape=jax.ShapeDtypeStruct((images, half, columns), BF),
-        in_specs=[ANY, ANY, ANY],
-        out_specs=VMEM,
-        scratch_shapes=[
-            pltpu.VMEM(tokens.shape, BF),
-            pltpu.VMEM(w_own.shape, BF),
-            pltpu.VMEM(w_other.shape, BF),
-            pltpu.SemaphoreType.DMA((5,)),
-        ],
+        in_specs=[VMEM, VMEM, ANY],
+        out_specs=VMEM,
+        scratch_shapes=[pltpu.VMEM(w_other.shape, BF), pltpu.SemaphoreType.DMA((2,))],
         compiler_params=params(12),
         cost_estimate=cost(2 * images * half * width * columns, 4 * 1024 * 1024),
         name="inner_part",
@@ -167,32 +155,28 @@
 
 
 def heads_kernel(
-    mine, theirs, w_own, w_other, inner_mine, inner_theirs, out, rows, rows_p, kept, kept_p, sems
+    mine, theirs, w_own, w_other, inner_mine, inner_theirs, out, kept, kept_p, sems
 ):
-    width, wide = rows.shape[-1], w_own.shape[1]
+    width, wide = mine.shape[-1], w_own.shape[1]
     half = out.shape[1] // 2
     copies = [
-        pltpu.make_async_copy(mine, rows, sems.at[0]),
-        pltpu.make_async_copy(w_own, kept, sems.at[1]),
-        pltpu.make_async_copy(w_other, kept_p, sems.at[2]),
-        pltpu.make_async_copy(theirs, rows_p, sems.at[3]),
-        pltpu.make_async_copy(inner_mine, out.at[:, :half, wide:], sems.at[4]),
-        pltpu.make_async_copy(inner_theirs, out.at[:, half:, wide:], sems.at[5]),
+        pltpu.make_async_copy(w_own, kept, sems.at[0]),
+        pltpu.make_async_copy(w_other, kept_p, sems.at[1]),
+        pltpu.make_async_copy(inner_mine, out.at[:, :half, wide:], sems.at[2]),
+        pltpu.make_async_copy(inner_theirs, out.at[:, half:, wide:], sems.at[3]),
     ]
     for copy in copies:
         copy.start()
     cols = width // 2
     copies[0].wait()
+    left = mine[...].reshape(-1, width)
+    own = dot(left[:, :cols], kept[...])
     copies[1].wait()
-    left = rows[...].reshape(-1, width)
-    own = dot(left[:, :cols], kept[...])
-    copies[2].wait()
     store(out, own + dot(left[:, cols:], kept_p[...]), 0, slice(0, wide))
-    copies[3].wait()
-    left = rows_p[...].reshape(-1, width)
+    left = theirs[...].reshape(-1, width)
     value = dot(left[:, :cols], kept[...]) + dot(left[:, cols:], kept_p[...])
     store(out, value, half, slice(0, wide))
-    for copy in copies[4:]:
+    for copy in copies[2:]:
         copy.wait()
 
 
@@ -202,11 +186,9 @@
     return pl.pallas_call(
         heads_kernel,
         out_shape=jax.ShapeDtypeStruct((images, 2 * half, wide + inner_mine.shape[2]), BF),
-        in_specs=[ANY, ANY, ANY, ANY, ANY, ANY],
-        out_specs=VMEM,
-        scratch_shapes=[pltpu.VMEM(mine.shape, BF)] * 2
-        + [pltpu.VMEM(w_own.shape, BF)] * 2
-        + [pltpu.SemaphoreType.DMA((6,))],
+        in_specs=[VMEM, VMEM, ANY, ANY, ANY, ANY],
+        out_specs=VMEM,
+        scratch_shapes=[pltpu.VMEM(w_own.shape, BF)] * 2 + [pltpu.SemaphoreType.DMA((4,))],
         compiler_params=params(12),
         cost_estimate=cost(4 * images * half * width * wide, 4 * 1024 * 1024),
         name="heads_part",
@@ -262,26 +244,16 @@
     )(arrived, bias, scale)
 
 
-def output_kernel(part, features, w_own, w_other, out, rows, kept_own, kept_other, sems):
-    images, half, width = rows.shape
-    cols = kept_own.shape[1]
-    copies = [
-        pltpu.make_async_copy(
-            features.at[:, part * half : (part + 1) * half], rows, sems.at[0]
-        ),
-        pltpu.make_async_copy(w_own, kept_own, sems.at[1]),
-        pltpu.make_async_copy(w_other, kept_other, sems.at[2]),
-    ]
-    for copy in copies:
-        copy.start()
-    copies[0].wait()
-    left = rows[...].reshape(images * half, width)
-    for n, kept in enumerate((kept_own, kept_other)):
-        copies[n + 1].wait()
+def output_kernel(part, features, w_own, w_other, out):
+    images, half, _ = out.shape
+    cols = w_own.shape[1]
+    left = features[:, part * half : (part + 1) * half].reshape(images * half, -1)
+    for n, weights in enumerate((w_own, w_other)):
         for m in range(2):
             at = slice(m * cols // 2, (m + 1) * cols // 2)
-            value = dot(left, kept[:, at]).astype(out.dtype).reshape(images, half, cols // 2)
-            out[:, :, n * cols + m * cols // 2 : n * cols + (m + 1) * cols // 2] = value
+            value = dot(left, weights[:, at]).astype(out.dtype)
+            to = slice(n * cols + m * cols // 2, n * cols + (m + 1) * cols // 2)
+            out[:, :, to] = value.reshape(images, half, cols // 2)
 
 
 def output(features, w_own, w_other, part, kind):
@@ -290,14 +262,8 @@
     return pl.pallas_call(
         functools.partial(output_kernel, part),
         out_shape=jax.ShapeDtypeStruct((images, half, 2 * cols), kind),
-        in_specs=[ANY] * 3,
-        out_specs=VMEM,
-        scratch_shapes=[
-            pltpu.VMEM((images, half, width), BF),
-            pltpu.VMEM(w_own.shape, BF),
-            pltpu.VMEM(w_other.shape, BF),
-            pltpu.SemaphoreType.DMA((3,)),
-        ],
+        in_specs=[VMEM] * 3,
+        out_specs=VMEM,
         compiler_params=params(16),
         cost_estimate=cost(4 * images * half * width * cols, 4 * 1024 * 1024),
         name="output_sent" if part else "output_kept",

time: 138 us -> 137 us (level)
  waiting for transfers between devices: 43.9 us -> 42.4 us
    pallas_call x2, Pallas kernels: 4.93 us -> 7.03 us  [inner_part(): pl.pallas_call(inner_kernel, out_shape=jax.ShapeDtypeStruct((images, half...]
    ppermute x6, waiting for transfers between devices: 12.2 us -> 10.7 us  [partner(): return lax.ppermute(array, axis, [(0, 1), (1, 0)])]
  transfers between devices with their start and end apart: 8 -> 8, of which waited for: 6 -> 6; matrix products, arithmetic and copies ran while one was open for 1% -> 1% of each run, Pallas kernels for 8% -> 9%
where the time goes in v1:
time: 137 us; the launch traced here: 134 us
  blocking collectives  48.1 us (35%)
  waiting for transfers between devices  42.4 us (31%)
  starting transfers between devices  23.7 us (17%)
  Pallas kernels  15.5 us (11%)
  local copies, waits for them, and re-layouts  3.74 us (3%)
    all_to_all x1, blocking collectives, exchange(): return lax.all_to_all(pieces, axes, split_axis=0, concat_axis=0, tiled=True)  34 us
    all_to_all x2, waiting for transfers between devices, exchange(): return lax.all_to_all(pieces, axes, split_axis=0, concat_axis=0, tiled=True)  31.7 us
    all_to_all x2, starting transfers between devices, exchange(): return lax.all_to_all(pieces, axes, split_axis=0, concat_axis=0, tiled=True)  16.8 us
    all_gather x1, blocking collectives, block(): features = lax.all_gather(features, 'y', axis=0, tiled=False)  14.1 us
    ppermute x6, waiting for transfers between devices, partner(): return lax.ppermute(array, axis, [(0, 1), (1, 0)])  10.7 us
    pallas_call x2, Pallas kernels, inner_part(): pl.pallas_call(inner_kernel, out_shape=jax.ShapeDtypeStruct((images, half...  7.03 us
    ppermute x6, starting transfers between devices, partner(): return lax.ppermute(array, axis, [(0, 1), (1, 0)])  6.9 us
    unnamed x21, local copies, waits for them, and re-layouts  3.61 us
  transfers between devices with their start and end apart: 8, of which 6 were waited for; matrix products, arithmetic and copies ran while one was open for 1% of the time, Pallas kernels for 9%

profile of v1, /device:TPU:8, one launch (start us, length us, event | category | flops | bytes accessed | tf_op | source)
XLA Modules:
  0.0 134.2 jit_solution(13741405356068701064)
XLA Ops:
  0.0 3.0 %collective-permute-start = (bf16[4,6144]{1,0:T(4,128)(2,1)}, bf16[4,6144]{1,0:T(4,128)(2,1)S(1)}, u32[]{:S(2)}, u32[]{:S(2)}) collective-permute-start(bf16[4,6144]{1,0:T(4,128)(2,1)} %tokens.3), channel_id=1, source_target_pairs={{0,2},{2,0},{1,3},{3,1},{4,6},{6,4},{5,7},{7,5},{8,10},{10,8},{9,1... | collective-permute-start | bytes 147464 | tf_op jit(solution)/shard_map/ppermute | solution.py:30
  3.0 0.0 copy-start.1
  3.0 0.8 copy-done.1
  3.9 0.0 copy-start.3
  3.9 0.7 copy-done.3
  4.6 0.0 copy-start.6
  4.6 0.4 norm_own.1
  5.0 0.8 collective-permute-done.beside
  5.8 0.0 copy-start.7
  5.8 1.2 normed_pieces.1
  7.0 0.0 copy-start.8
  7.0 0.0 copy-start.5
  7.0 11.8 %all-to-all-start = ((bf16[32,8,1536]{2,1,0:T(8,128)(2,1)}), bf16[32,8,1536]{2,1,0:T(8,128)(2,1)S(1)}, u32[]{:S(2)}, u32[]{:S(2)}) async-start(bf16[32,8,1536]{2,1,0:T(8,128)(2,1)} %normed_pieces.1), calls=%async_computation | async-start | bytes 1572864 | tf_op jit(solution)/shard_map/all_to_all | solution.py:34
  18.9 1.6 %collective-permute-start.3 = (bf16[768,768]{1,0:T(8,128)(2,1)}, bf16[768,768]{1,0:T(8,128)(2,1)}, u32[]{:S(2)}, u32[]{:S(2)}) collective-permute-start(bf16[768,768]{1,0:T(8,128)(2,1)} %w_own.3), channel_id=1, source_target_pairs={{0,128},{128,0},{1,129},{129,1},{2,130},{130,2},{3,131},{131,3},{4... | collective-permute-start | bytes 3538952 | tf_op jit(solution)/shard_map/ppermute | solution.py:30
  20.5 19.8 %all-to-all-done.rows.mine = bf16[32,8,1536]{2,1,0:T(8,128)(2,1)S(1)} async-done(((bf16[32,8,1536]{2,1,0:T(8,128)(2,1)}), bf16[32,8,1536]{2,1,0:T(8,128)(2,1)S(1)}, u32[]{:S(2)}, u32[]{:S(2)}) %all-to-all-start) | async-done | bytes 786464 | tf_op jit(solution)/shard_map/all_to_all | solution.py:34
  40.2 0.0 collective-permute-start.1
  40.2 0.0 copy-done.6
  40.3 0.0 copy-done.7
  40.4 0.0 copy-done.8
  40.4 1.5 %collective-permute-start.2 = (bf16[768,384]{1,0:T(8,128)(2,1)S(1)}, bf16[768,384]{1,0:T(8,128)(2,1)S(1)}, u32[]{:S(2)}, u32[]{:S(2)}) collective-permute-start(bf16[768,384]{1,0:T(8,128)(2,1)S(1)} %constant_dynamic-update-slice_fusion.w_own), channel_id=1, source_target_pairs={{0,128},{128,0},{1,129},{129,1},{2,130},{130,2},{3,131},{131,3},{4... | collective-permute-start | bytes 1769480 | tf_op jit(solution)/shard_map/ppermute | solution.py:30
  41.9 0.9 constant_dynamic-update-slice_fusion.4
  42.9 0.0 copy-done.5
  42.9 0.1 constant_dynamic-update-slice_fusion.3.w_own
  43.0 0.7 collective-permute-start.4
  43.7 3.3 %collective-permute-done.3.w_other = bf16[768,768]{1,0:T(8,128)(2,1)} collective-permute-done((bf16[768,768]{1,0:T(8,128)(2,1)}, bf16[768,768]{1,0:T(8,128)(2,1)}, u32[]{:S(2)}, u32[]{:S(2)}) %collective-permute-start.3) | collective-permute-done | bytes 1179680 | tf_op jit(solution)/shard_map/ppermute | solution.py:30
  47.0 3.5 %inner_part.2.inner_mine = bf16[4,64,768]{2,1,0:T(8,128)(2,1)S(1)} custom-call(bf16[32,8,1536]{2,1,0:T(8,128)(2,1)S(1)} %all-to-all-done.rows.mine, bf16[768,768]{1,0:T(8,128)(2,1)} %w_own.3, bf16[768,768]{1,0:T(8,128)(2,1)} %collective-permute-done.3.w_other), custom_call_target="tpu_custom_call" | custom-call | flops 603979776 | bytes 4194304 | tf_op jit(solution)/shard_map/inner_part/pallas_call | solution.py:145
  50.5 0.0 collective-permute-done.1.rows.theirs
  50.5 3.5 %inner_part.3.inner_theirs = bf16[4,64,768]{2,1,0:T(8,128)(2,1)S(1)} custom-call(bf16[32,8,1536]{2,1,0:T(8,128)(2,1)S(1)} %collective-permute-done.1.rows.theirs, bf16[768,768]{1,0:T(8,128)(2,1)} %w_own.3, bf16[768,768]{1,0:T(8,128)(2,1)} %collective-permute-done.3.w_other), custom_call_target="tpu_custom_call" | custom-call | flops 603979776 | bytes 4194304 | tf_op jit(solution)/shard_map/inner_part/pallas_call | solution.py:145
  54.0 5.5 %collective-permute-done.2.w_other = bf16[768,384]{1,0:T(8,128)(2,1)S(1)} collective-permute-done((bf16[768,384]{1,0:T(8,128)(2,1)S(1)}, bf16[768,384]{1,0:T(8,128)(2,1)S(1)}, u32[]{:S(2)}, u32[]{:S(2)}) %collective-permute-start.2) | collective-permute-done | bytes 589856 | tf_op jit(solution)/shard_map/ppermute | solution.py:30
  59.5 1.4 %heads_part.1 = bf16[4,128,1152]{2,1,0:T(8,128)(2,1)S(1)} custom-call(bf16[32,8,1536]{2,1,0:T(8,128)(2,1)S(1)} %all-to-all-done.rows.mine, bf16[32,8,1536]{2,1,0:T(8,128)(2,1)S(1)} %collective-permute-done.1.rows.theirs, bf16[768,384]{1,0:T(8,128)(2,1)S(1)} %constant_dynamic-update-slice_fusion.w_own, bf16[768,384]{1,0:T(8,128)(2,1)S(1)} %collective-permute-done.2.w_other, ...), custom_call_target="tpu_custom_call" | custom-call | flops 603979776 | bytes 4194304 | tf_op jit(solution)/shard_map/heads_part/pallas_call | solution.py:186
  60.9 0.0 copy-start
  60.9 1.0 copy-done
  61.9 0.0 copy-start.4
  61.9 4.9 %all-to-all-start.1 = ((bf16[4,128,1152]{2,1,0:T(8,128)(2,1)}), bf16[4,128,1152]{2,1,0:T(8,128)(2,1)}, u32[]{:S(2)}, u32[]{:S(2)}) async-start(bf16[4,128,1152]{2,1,0:T(8,128)(2,1)} %copy-done), calls=%async_computation.1 | async-start | bytes 2359296 | tf_op jit(solution)/shard_map/all_to_all | solution.py:34
  67.5 12.0 %all-to-all-done.1.arrived = bf16[4,128,1152]{2,1,0:T(8,128)(2,1)} async-done(((bf16[4,128,1152]{2,1,0:T(8,128)(2,1)}), bf16[4,128,1152]{2,1,0:T(8,128)(2,1)}, u32[]{:S(2)}, u32[]{:S(2)}) %all-to-all-start.1) | async-done | bytes 1179680 | tf_op jit(solution)/shard_map/all_to_all | solution.py:34
  79.5 0.0 copy-done.4
  79.5 2.1 %middle.1 = bf16[1,128,896]{2,1,0:T(8,128)(2,1)S(1)} custom-call(bf16[4,128,1152]{2,1,0:T(8,128)(2,1)} %all-to-all-done.1.arrived, f32[768]{0:T(1024)S(1)} %copy-done.4, f32[1]{0:T(128)S(6)} %div.3.scale), custom_call_target="tpu_custom_call" | custom-call | flops 5898240 | bytes 2097152 | tf_op jit(solution)/shard_map/middle/pallas_call | solution.py:235
  81.6 14.1 %all_gather.3.features = bf16[4,128,896]{2,1,0:T(8,128)(2,1)S(1)} all-gather(bf16[1,128,896]{2,1,0:T(8,128)(2,1)S(1)} %middle.1), channel_id=1, replica_groups=mesh['xl'=2,'y'=4,'z'=8,'xh'=2,'c'=2] {'y'}, dimensions={0}, use_global_device_ids=true | all-gather | bytes 1146880 | tf_op jit(solution)/shard_map/all_gather | solution.py:347
  95.7 0.0 collective-permute-done.4.w_other
  95.7 1.2 output_sent.1
  96.9 0.1 collective-permute-start.5
  97.0 1.2 output_kept.1.kept
  98.2 1.1 collective-permute-done.5.received
  99.3 0.2 combine.1
  99.5 0.0 copy-start.2
  99.5 34.0 %all_to_all.15.arrived = bf16[64,4,1536]{2,1,0:T(4,128)(2,1)S(1)} all-to-all(bf16[64,4,1536]{2,1,0:T(4,128)(2,1)S(1)} %combine.1), channel_id=1, replica_groups=mesh['xl'=2,'y'=4,'z'=8,'xh'=2,'c'=2] {'xh','z','y'}, dimensions={0} | all-to-all | bytes 1572864 | tf_op jit(solution)/shard_map/all_to_all | solution.py:34
  133.4 0.0 copy-done.2
  133.4 0.7 finish.1
  (3 shorter events, 0.1 us)
Async XLA Ops:
  0.0 5.8 %collective-permute-start = (bf16[4,6144]{1,0:T(4,128)(2,1)}, bf16[4,6144]{1,0:T(4,128)(2,1)S(1)}, u32[]{:S(2)}, u32[]{:S(2)}) collective-permute-start(bf16[4,6144]{1,0:T(4,128)(2,1)} %tokens.3), channel_id=1, source_target_pairs={{0,2},{2,0},{1,3},{3,1},{4,6},{6,4},{5,7},{7,5},{8,10},{10,8},{9,1... | collective-permute-start | bytes 147464 | tf_op jit(solution)/shard_map/ppermute | solution.py:30
  3.0 0.8 copy-start.1
  3.9 0.7 copy-start.3
  4.6 35.7 %copy-start.6 = (bf16[768,128]{1,0:T(8,128)(2,1)S(1)}, bf16[768,128]{1,0:T(8,128)(2,1)}, u32[]{:S(2)}) copy-start(bf16[768,128]{1,0:T(8,128)(2,1)} %param.12) | copy-start | bytes 589828
  5.8 34.5 %copy-start.7 = (bf16[768,128]{1,0:T(8,128)(2,1)S(1)}, bf16[768,128]{1,0:T(8,128)(2,1)}, u32[]{:S(2)}) copy-start(bf16[768,128]{1,0:T(8,128)(2,1)} %param.13) | copy-start | bytes 589828
  7.0 33.3 %copy-start.8 = (bf16[768,128]{1,0:T(8,128)(2,1)S(1)}, bf16[768,128]{1,0:T(8,128)(2,1)}, u32[]{:S(2)}) copy-start(bf16[768,128]{1,0:T(8,128)(2,1)} %param.14) | copy-start | bytes 589828
  7.0 35.8 %copy-start.5 = (bf16[768,768]{1,0:T(8,128)(2,1)S(1)}, bf16[768,768]{1,0:T(8,128)(2,1)}, u32[]{:S(2)}) copy-start(bf16[768,768]{1,0:T(8,128)(2,1)} %param.18) | copy-start | bytes 3538948
  7.0 33.2 %all-to-all-start = ((bf16[32,8,1536]{2,1,0:T(8,128)(2,1)}), bf16[32,8,1536]{2,1,0:T(8,128)(2,1)S(1)}, u32[]{:S(2)}, u32[]{:S(2)}) async-start(bf16[32,8,1536]{2,1,0:T(8,128)(2,1)} %normed_pieces.1), calls=%async_computation | async-start | bytes 1572864 | tf_op jit(solution)/shard_map/all_to_all | solution.py:34
  18.9 28.1 %collective-permute-start.3 = (bf16[768,768]{1,0:T(8,128)(2,1)}, bf16[768,768]{1,0:T(8,128)(2,1)}, u32[]{:S(2)}, u32[]{:S(2)}) collective-permute-start(bf16[768,768]{1,0:T(8,128)(2,1)} %w_own.3), channel_id=1, source_target_pairs={{0,128},{128,0},{1,129},{129,1},{2,130},{130,2},{3,131},{131,3},{4... | collective-permute-start | bytes 3538952 | tf_op jit(solution)/shard_map/ppermute | solution.py:30
  40.2 10.3 %collective-permute-start.1 = (bf16[32,8,1536]{2,1,0:T(8,128)(2,1)S(1)}, bf16[32,8,1536]{2,1,0:T(8,128)(2,1)S(1)}, u32[]{:S(2)}, u32[]{:S(2)}) collective-permute-start(bf16[32,8,1536]{2,1,0:T(8,128)(2,1)S(1)} %all-to-all-done.rows.mine), channel_id=1, source_target_pairs={{0,1},{1,0},{2,3},{3,2},{4,5},{5,4},{6,7},{7,6},{8,9},{9,8},{10,11... | collective-permute-start | bytes 2359304 | tf_op jit(solution)/shard_map/ppermute | solution.py:30
  40.4 19.1 %collective-permute-start.2 = (bf16[768,384]{1,0:T(8,128)(2,1)S(1)}, bf16[768,384]{1,0:T(8,128)(2,1)S(1)}, u32[]{:S(2)}, u32[]{:S(2)}) collective-permute-start(bf16[768,384]{1,0:T(8,128)(2,1)S(1)} %constant_dynamic-update-slice_fusion.w_own), channel_id=1, source_target_pairs={{0,128},{128,0},{1,129},{129,1},{2,130},{130,2},{3,131},{131,3},{4... | collective-permute-start | bytes 1769480 | tf_op jit(solution)/shard_map/ppermute | solution.py:30
  43.0 52.7 %collective-permute-start.4 = (bf16[896,768]{1,0:T(8,128)(2,1)S(1)}, bf16[896,768]{1,0:T(8,128)(2,1)S(1)}, u32[]{:S(2)}, u32[]{:S(2)}) collective-permute-start(bf16[896,768]{1,0:T(8,128)(2,1)S(1)} %constant_dynamic-update-slice_fusion.3.w_own), channel_id=1, source_target_pairs={{0,128},{128,0},{1,129},{129,1},{2,130},{130,2},{3,131},{131,3},{4... | collective-permute-start | bytes 4128776 | tf_op jit(solution)/shard_map/ppermute | solution.py:30
  60.9 1.0 copy-start
  61.9 17.5 %copy-start.4 = (f32[768]{0:T(1024)S(1)}, f32[768]{0:T(1024)}, u32[]{:S(2)}) copy-start(f32[768]{0:T(1024)} %bias.1) | copy-start | bytes 9220
  61.9 17.5 %all-to-all-start.1 = ((bf16[4,128,1152]{2,1,0:T(8,128)(2,1)}), bf16[4,128,1152]{2,1,0:T(8,128)(2,1)}, u32[]{:S(2)}, u32[]{:S(2)}) async-start(bf16[4,128,1152]{2,1,0:T(8,128)(2,1)} %copy-done), calls=%async_computation.1 | async-start | bytes 2359296 | tf_op jit(solution)/shard_map/all_to_all | solution.py:34
  96.9 2.4 %collective-permute-start.5 = (bf16[4,64,1536]{2,1,0:T(8,128)(2,1)S(1)}, bf16[4,64,1536]{2,1,0:T(8,128)(2,1)S(1)}, u32[]{:S(2)}, u32[]{:S(2)}) collective-permute-start(bf16[4,64,1536]{2,1,0:T(8,128)(2,1)S(1)} %output_sent.1), channel_id=1, source_target_pairs={{0,1},{1,0},{2,3},{3,2},{4,5},{5,4},{6,7},{7,6},{8,9},{9,8},{10,11... | collective-permute-start | bytes 2359304 | tf_op jit(solution)/shard_map/ppermute | solution.py:30
  99.5 34.0 %copy-start.2 = (bf16[4,6144]{1,0:T(4,128)(2,1)S(1)}, bf16[4,6144]{1,0:T(4,128)(2,1)}, u32[]{:S(2)}) copy-start(bf16[4,6144]{1,0:T(4,128)(2,1)} %tokens.3) | copy-start | bytes 147460

commit v2 on v1

--- a/solution.py
+++ b/solution.py
@@ -244,56 +244,62 @@
     )(arrived, bias, scale)
 
 
-def output_kernel(part, features, w_own, w_other, out):
+def output_kernel(part, features, *refs):
+    weights, out = refs[:-1], refs[-1]
     images, half, _ = out.shape
-    cols = w_own.shape[1]
+    cols = weights[0].shape[1]
     left = features[:, part * half : (part + 1) * half].reshape(images * half, -1)
-    for n, weights in enumerate((w_own, w_other)):
+    for n, source in enumerate(weights):
         for m in range(2):
             at = slice(m * cols // 2, (m + 1) * cols // 2)
-            value = dot(left, weights[:, at]).astype(out.dtype)
+            value = dot(left, source[:, at]).astype(out.dtype)
             to = slice(n * cols + m * cols // 2, n * cols + (m + 1) * cols // 2)
             out[:, :, to] = value.reshape(images, half, cols // 2)
 
 
-def output(features, w_own, w_other, part, kind):
+def output(features, weights, part, kind):
     images, patches, width = features.shape
-    half, cols = patches // 2, w_own.shape[1]
+    half, cols = patches // 2, weights[0].shape[1] * len(weights)
     return pl.pallas_call(
         functools.partial(output_kernel, part),
-        out_shape=jax.ShapeDtypeStruct((images, half, 2 * cols), kind),
-        in_specs=[VMEM] * 3,
+        out_shape=jax.ShapeDtypeStruct((images, half, cols), kind),
+        in_specs=[VMEM] * (1 + len(weights)),
         out_specs=VMEM,
         compiler_params=params(16),
-        cost_estimate=cost(4 * images * half * width * cols, 4 * 1024 * 1024),
+        cost_estimate=cost(2 * images * half * width * cols, 2 * 1024 * 1024),
         name="output_sent" if part else "output_kept",
-    )(features, w_own, w_other)
-
-
-def combine_kernel(n_xh, kept, received, out):
+    )(features, *weights)
+
+
+def combine_kernel(n_xh, kept, received, received_p, out):
     images, half, _ = kept.shape
     n_z = half // 8
     count = 8 // n_xh
     for y in range(images):
         for z in range(n_z):
             at = slice(z * 8, (z + 1) * 8)
-            value = kept[y, at] + received[y, at].astype(F32)
-            for xh in range(n_xh):
-                out[(xh * n_z + z) * images + y] = value[xh * count : (xh + 1) * count].astype(BF)
-
-
-def combine(kept, received, n_xh):
+            for n, source in enumerate((received, received_p)):
+                cols = source.shape[-1]
+                to = slice(n * cols, (n + 1) * cols)
+                value = kept[y, at, to] + source[y, at].astype(F32)
+                for xh in range(n_xh):
+                    out[(xh * n_z + z) * images + y, :, to] = value[
+                        xh * count : (xh + 1) * count
+                    ].astype(BF)
+
+
+def combine(kept, received, received_p, n_xh):
     images, half, width = kept.shape
     count = 8 // n_xh
     return pl.pallas_call(
         functools.partial(combine_kernel, n_xh),
         out_shape=jax.ShapeDtypeStruct((images * half // count, count, width), BF),
-        in_specs=[VMEM] * 2,
+        in_specs=[VMEM] * 3,
         out_specs=VMEM,
         compiler_params=params(8),
         cost_estimate=cost(kept.size, 4 * 1024 * 1024),
         name="combine",
-    )(kept, received)
+    )(kept, received, received_p)
 
 
 def finish_kernel(n_y, arrived, tokens, out):
@@ -345,9 +351,10 @@
     scale = temper / math.sqrt(HEAD)
     features = middle(arrived, bias_inner, scale)[0]
     features = lax.all_gather(features, "y", axis=0, tiled=False)
-    sent = partner(output(features, w_out, w_out_p, 1, BF), "c")
-    kept = output(features, w_out, w_out_p, 0, F32)
-    pieces = combine(kept, sent, n_xh)
+    sent = partner(output(features, (w_out,), 1, BF), "c")
+    sent_p = partner(output(features, (w_out_p,), 1, BF), "c")
+    kept = output(features, (w_out, w_out_p), 0, F32)
+    pieces = combine(kept, sent, sent_p, n_xh)
     arrived = exchange(pieces, ("xh", "z", "y"))
     return finish(arrived, tokens, n_y)
 

time: 137 us -> 137 us (level)
    ppermute x6 -> x7, waiting for transfers between devices: 10.7 us -> 9.79 us  [partner(): return lax.ppermute(array, axis, [(0, 1), (1, 0)])]
    ppermute x6 -> x7, starting transfers between devices: 6.9 us -> 7.47 us  [partner(): return lax.ppermute(array, axis, [(0, 1), (1, 0)])]
  transfers between devices with their start and end apart: 8 -> 9, of which waited for: 6 -> 6; matrix products, arithmetic and copies ran while one was open for 1% -> 1% of each run, Pallas kernels for 9% -> 10%
where the time goes in v2:
time: 137 us; the launch traced here: 135 us
  blocking collectives  48.8 us (36%)
  waiting for transfers between devices  41.5 us (30%)
  starting transfers between devices  24.2 us (18%)
  Pallas kernels  15.6 us (11%)
  local copies, waits for them, and re-layouts  3.73 us (3%)
    all_to_all x1, blocking collectives, exchange(): return lax.all_to_all(pieces, axes, split_axis=0, concat_axis=0, tiled=True)  34.7 us
    all_to_all x2, waiting for transfers between devices, exchange(): return lax.all_to_all(pieces, axes, split_axis=0, concat_axis=0, tiled=True)  31.7 us
    all_to_all x2, starting transfers between devices, exchange(): return lax.all_to_all(pieces, axes, split_axis=0, concat_axis=0, tiled=True)  16.8 us
    all_gather x1, blocking collectives, block(): features = lax.all_gather(features, 'y', axis=0, tiled=False)  14.1 us
    ppermute x7, waiting for transfers between devices, partner(): return lax.ppermute(array, axis, [(0, 1), (1, 0)])  9.79 us
    ppermute x7, starting transfers between devices, partner(): return lax.ppermute(array, axis, [(0, 1), (1, 0)])  7.47 us
    pallas_call x2, Pallas kernels, inner_part(): pl.pallas_call(inner_kernel, out_shape=jax.ShapeDtypeStruct((images, half...  7.03 us
    unnamed x21, local copies, waits for them, and re-layouts  3.6 us
  transfers between devices with their start and end apart: 9, of which 6 were waited for; matrix products, arithmetic and copies ran while one was open for 1% of the time, Pallas kernels for 10%

profile of v2, /device:TPU:8, one launch (start us, length us, event | category | flops | bytes accessed | tf_op | source)
XLA Modules:
  0.0 134.7 jit_solution(45079596697402835)
XLA Ops:
  0.0 3.0 %collective-permute-start = (bf16[4,6144]{1,0:T(4,128)(2,1)}, bf16[4,6144]{1,0:T(4,128)(2,1)S(1)}, u32[]{:S(2)}, u32[]{:S(2)}) collective-permute-start(bf16[4,6144]{1,0:T(4,128)(2,1)} %tokens.3), channel_id=1, source_target_pairs={{0,2},{2,0},{1,3},{3,1},{4,6},{6,4},{5,7},{7,5},{8,10},{10,8},{9,1... | collective-permute-start | bytes 147464 | tf_op jit(solution)/shard_map/ppermute | solution.py:30
  3.0 0.0 copy-start.1
  3.0 0.8 copy-done.1
  3.9 0.0 copy-start.3
  3.9 0.7 copy-done.3
  4.6 0.4 norm_own.1
  5.0 0.8 collective-permute-done.beside
  5.8 0.0 copy-start.7
  5.8 1.2 normed_pieces.1
  7.0 0.0 copy-start.5
  7.0 11.8 %all-to-all-start = ((bf16[32,8,1536]{2,1,0:T(8,128)(2,1)}), bf16[32,8,1536]{2,1,0:T(8,128)(2,1)S(1)}, u32[]{:S(2)}, u32[]{:S(2)}) async-start(bf16[32,8,1536]{2,1,0:T(8,128)(2,1)} %normed_pieces.1), calls=%async_computation | async-start | bytes 1572864 | tf_op jit(solution)/shard_map/all_to_all | solution.py:34
  18.9 1.6 %collective-permute-start.3 = (bf16[768,768]{1,0:T(8,128)(2,1)}, bf16[768,768]{1,0:T(8,128)(2,1)}, u32[]{:S(2)}, u32[]{:S(2)}) collective-permute-start(bf16[768,768]{1,0:T(8,128)(2,1)} %w_own.3), channel_id=1, source_target_pairs={{0,128},{128,0},{1,129},{129,1},{2,130},{130,2},{3,131},{131,3},{4... | collective-permute-start | bytes 3538952 | tf_op jit(solution)/shard_map/ppermute | solution.py:30
  20.5 19.8 %all-to-all-done.rows.mine = bf16[32,8,1536]{2,1,0:T(8,128)(2,1)S(1)} async-done(((bf16[32,8,1536]{2,1,0:T(8,128)(2,1)}), bf16[32,8,1536]{2,1,0:T(8,128)(2,1)S(1)}, u32[]{:S(2)}, u32[]{:S(2)}) %all-to-all-start) | async-done | bytes 786464 | tf_op jit(solution)/shard_map/all_to_all | solution.py:34
  40.2 0.0 collective-permute-start.1
  40.3 0.0 copy-done.6
  40.3 0.0 copy-done.7
  40.4 0.0 copy-done.8
  40.4 1.5 %collective-permute-start.2 = (bf16[768,384]{1,0:T(8,128)(2,1)S(1)}, bf16[768,384]{1,0:T(8,128)(2,1)S(1)}, u32[]{:S(2)}, u32[]{:S(2)}) collective-permute-start(bf16[768,384]{1,0:T(8,128)(2,1)S(1)} %constant_dynamic-update-slice_fusion.w_own), channel_id=1, source_target_pairs={{0,128},{128,0},{1,129},{129,1},{2,130},{130,2},{3,131},{131,3},{4... | collective-permute-start | bytes 1769480 | tf_op jit(solution)/shard_map/ppermute | solution.py:30
  41.9 0.9 constant_dynamic-update-slice_fusion.4
  42.9 0.0 copy-done.5
  42.9 0.1 constant_dynamic-update-slice_fusion.3.refs_0_
  43.0 0.7 collective-permute-start.4
  43.7 3.3 %collective-permute-done.3.w_other = bf16[768,768]{1,0:T(8,128)(2,1)} collective-permute-done((bf16[768,768]{1,0:T(8,128)(2,1)}, bf16[768,768]{1,0:T(8,128)(2,1)}, u32[]{:S(2)}, u32[]{:S(2)}) %collective-permute-start.3) | collective-permute-done | bytes 1179680 | tf_op jit(solution)/shard_map/ppermute | solution.py:30
  47.0 3.5 %inner_part.2.inner_mine = bf16[4,64,768]{2,1,0:T(8,128)(2,1)S(1)} custom-call(bf16[32,8,1536]{2,1,0:T(8,128)(2,1)S(1)} %all-to-all-done.rows.mine, bf16[768,768]{1,0:T(8,128)(2,1)} %w_own.3, bf16[768,768]{1,0:T(8,128)(2,1)} %collective-permute-done.3.w_other), custom_call_target="tpu_custom_call" | custom-call | flops 603979776 | bytes 4194304 | tf_op jit(solution)/shard_map/inner_part/pallas_call | solution.py:145
  50.5 0.0 collective-permute-done.1.rows.theirs
  50.5 3.5 %inner_part.3.inner_theirs = bf16[4,64,768]{2,1,0:T(8,128)(2,1)S(1)} custom-call(bf16[32,8,1536]{2,1,0:T(8,128)(2,1)S(1)} %collective-permute-done.1.rows.theirs, bf16[768,768]{1,0:T(8,128)(2,1)} %w_own.3, bf16[768,768]{1,0:T(8,128)(2,1)} %collective-permute-done.3.w_other), custom_call_target="tpu_custom_call" | custom-call | flops 603979776 | bytes 4194304 | tf_op jit(solution)/shard_map/inner_part/pallas_call | solution.py:145
  54.0 5.5 %collective-permute-done.2.w_other = bf16[768,384]{1,0:T(8,128)(2,1)S(1)} collective-permute-done((bf16[768,384]{1,0:T(8,128)(2,1)S(1)}, bf16[768,384]{1,0:T(8,128)(2,1)S(1)}, u32[]{:S(2)}, u32[]{:S(2)}) %collective-permute-start.2) | collective-permute-done | bytes 589856 | tf_op jit(solution)/shard_map/ppermute | solution.py:30
  59.5 1.4 %heads_part.1 = bf16[4,128,1152]{2,1,0:T(8,128)(2,1)S(1)} custom-call(bf16[32,8,1536]{2,1,0:T(8,128)(2,1)S(1)} %all-to-all-done.rows.mine, bf16[32,8,1536]{2,1,0:T(8,128)(2,1)S(1)} %collective-permute-done.1.rows.theirs, bf16[768,384]{1,0:T(8,128)(2,1)S(1)} %constant_dynamic-update-slice_fusion.w_own, bf16[768,384]{1,0:T(8,128)(2,1)S(1)} %collective-permute-done.2.w_other, ...), custom_call_target="tpu_custom_call" | custom-call | flops 603979776 | bytes 4194304 | tf_op jit(solution)/shard_map/heads_part/pallas_call | solution.py:186
  60.9 0.0 copy-start
  60.9 1.0 copy-done
  61.9 4.9 %all-to-all-start.1 = ((bf16[4,128,1152]{2,1,0:T(8,128)(2,1)}), bf16[4,128,1152]{2,1,0:T(8,128)(2,1)}, u32[]{:S(2)}, u32[]{:S(2)}) async-start(bf16[4,128,1152]{2,1,0:T(8,128)(2,1)} %copy-done), calls=%async_computation.1 | async-start | bytes 2359296 | tf_op jit(solution)/shard_map/all_to_all | solution.py:34
  67.5 11.9 %all-to-all-done.1.arrived = bf16[4,128,1152]{2,1,0:T(8,128)(2,1)} async-done(((bf16[4,128,1152]{2,1,0:T(8,128)(2,1)}), bf16[4,128,1152]{2,1,0:T(8,128)(2,1)}, u32[]{:S(2)}, u32[]{:S(2)}) %all-to-all-start.1) | async-done | bytes 1179680 | tf_op jit(solution)/shard_map/all_to_all | solution.py:34
  79.5 0.0 copy-done.4
  79.5 2.1 %middle.1 = bf16[1,128,896]{2,1,0:T(8,128)(2,1)S(1)} custom-call(bf16[4,128,1152]{2,1,0:T(8,128)(2,1)} %all-to-all-done.1.arrived, f32[768]{0:T(1024)S(1)} %copy-done.4, f32[1]{0:T(128)S(6)} %div.3.scale), custom_call_target="tpu_custom_call" | custom-call | flops 5898240 | bytes 2097152 | tf_op jit(solution)/shard_map/middle/pallas_call | solution.py:235
  81.6 14.1 %all_gather.3.features = bf16[4,128,896]{2,1,0:T(8,128)(2,1)S(1)} all-gather(bf16[1,128,896]{2,1,0:T(8,128)(2,1)S(1)} %middle.1), channel_id=1, replica_groups=mesh['xl'=2,'y'=4,'z'=8,'xh'=2,'c'=2] {'y'}, dimensions={0}, use_global_device_ids=true | all-gather | bytes 1146880 | tf_op jit(solution)/shard_map/all_gather | solution.py:353
  95.7 0.7 output_sent.2
  96.4 0.1 collective-permute-start.5
  96.5 0.0 collective-permute-done.4.refs_1_.refs_0_
  96.5 0.7 output_sent.3
  97.2 0.6 collective-permute-start.6
  97.7 1.2 output_kept.1.kept
  98.9 0.0 collective-permute-done.5.received
  98.9 0.2 collective-permute-done.6.received_p
  99.1 0.2 combine.1
  99.3 0.0 copy-start.2
  99.3 34.7 %all_to_all.15.arrived = bf16[64,4,1536]{2,1,0:T(4,128)(2,1)S(1)} all-to-all(bf16[64,4,1536]{2,1,0:T(4,128)(2,1)S(1)} %combine.1), channel_id=1, replica_groups=mesh['xl'=2,'y'=4,'z'=8,'xh'=2,'c'=2] {'xh','z','y'}, dimensions={0} | all-to-all | bytes 1572864 | tf_op jit(solution)/shard_map/all_to_all | solution.py:34
  134.0 0.0 copy-done.2
  134.0 0.7 finish.1
  (6 shorter events, 0.1 us)
Async XLA Ops:
  0.0 5.8 %collective-permute-start = (bf16[4,6144]{1,0:T(4,128)(2,1)}, bf16[4,6144]{1,0:T(4,128)(2,1)S(1)}, u32[]{:S(2)}, u32[]{:S(2)}) collective-permute-start(bf16[4,6144]{1,0:T(4,128)(2,1)} %tokens.3), channel_id=1, source_target_pairs={{0,2},{2,0},{1,3},{3,1},{4,6},{6,4},{5,7},{7,5},{8,10},{10,8},{9,1... | collective-permute-start | bytes 147464 | tf_op jit(solution)/shard_map/ppermute | solution.py:30
  3.0 0.8 copy-start.1
  3.9 0.7 copy-start.3
  4.6 35.7 %copy-start.6 = (bf16[768,128]{1,0:T(8,128)(2,1)S(1)}, bf16[768,128]{1,0:T(8,128)(2,1)}, u32[]{:S(2)}) copy-start(bf16[768,128]{1,0:T(8,128)(2,1)} %param.12) | copy-start | bytes 589828
  5.8 34.5 %copy-start.7 = (bf16[768,128]{1,0:T(8,128)(2,1)S(1)}, bf16[768,128]{1,0:T(8,128)(2,1)}, u32[]{:S(2)}) copy-start(bf16[768,128]{1,0:T(8,128)(2,1)} %param.13) | copy-start | bytes 589828
  7.0 33.3 %copy-start.8 = (bf16[768,128]{1,0:T(8,128)(2,1)S(1)}, bf16[768,128]{1,0:T(8,128)(2,1)}, u32[]{:S(2)}) copy-start(bf16[768,128]{1,0:T(8,128)(2,1)} %param.14) | copy-start | bytes 589828
  7.0 35.8 %copy-start.5 = (bf16[768,768]{1,0:T(8,128)(2,1)S(1)}, bf16[768,768]{1,0:T(8,128)(2,1)}, u32[]{:S(2)}) copy-start(bf16[768,768]{1,0:T(8,128)(2,1)} %param.18) | copy-start | bytes 3538948
  7.0 33.2 %all-to-all-start = ((bf16[32,8,1536]{2,1,0:T(8,128)(2,1)}), bf16[32,8,1536]{2,1,0:T(8,128)(2,1)S(1)}, u32[]{:S(2)}, u32[]{:S(2)}) async-start(bf16[32,8,1536]{2,1,0:T(8,128)(2,1)} %normed_pieces.1), calls=%async_computation | async-start | bytes 1572864 | tf_op jit(solution)/shard_map/all_to_all | solution.py:34
  18.9 28.1 %collective-permute-start.3 = (bf16[768,768]{1,0:T(8,128)(2,1)}, bf16[768,768]{1,0:T(8,128)(2,1)}, u32[]{:S(2)}, u32[]{:S(2)}) collective-permute-start(bf16[768,768]{1,0:T(8,128)(2,1)} %w_own.3), channel_id=1, source_target_pairs={{0,128},{128,0},{1,129},{129,1},{2,130},{130,2},{3,131},{131,3},{4... | collective-permute-start | bytes 3538952 | tf_op jit(solution)/shard_map/ppermute | solution.py:30
  40.2 10.3 %collective-permute-start.1 = (bf16[32,8,1536]{2,1,0:T(8,128)(2,1)S(1)}, bf16[32,8,1536]{2,1,0:T(8,128)(2,1)S(1)}, u32[]{:S(2)}, u32[]{:S(2)}) collective-permute-start(bf16[32,8,1536]{2,1,0:T(8,128)(2,1)S(1)} %all-to-all-done.rows.mine), channel_id=1, source_target_pairs={{0,1},{1,0},{2,3},{3,2},{4,5},{5,4},{6,7},{7,6},{8,9},{9,8},{10,11... | collective-permute-start | bytes 2359304 | tf_op jit(solution)/shard_map/ppermute | solution.py:30
  40.4 19.1 %collective-permute-start.2 = (bf16[768,384]{1,0:T(8,128)(2,1)S(1)}, bf16[768,384]{1,0:T(8,128)(2,1)S(1)}, u32[]{:S(2)}, u32[]{:S(2)}) collective-permute-start(bf16[768,384]{1,0:T(8,128)(2,1)S(1)} %constant_dynamic-update-slice_fusion.w_own), channel_id=1, source_target_pairs={{0,128},{128,0},{1,129},{129,1},{2,130},{130,2},{3,131},{131,3},{4... | collective-permute-start | bytes 1769480 | tf_op jit(solution)/shard_map/ppermute | solution.py:30
  43.0 53.5 %collective-permute-start.4 = (bf16[896,768]{1,0:T(8,128)(2,1)S(1)}, bf16[896,768]{1,0:T(8,128)(2,1)S(1)}, u32[]{:S(2)}, u32[]{:S(2)}) collective-permute-start(bf16[896,768]{1,0:T(8,128)(2,1)S(1)} %constant_dynamic-update-slice_fusion.3.refs_0_), channel_id=1, source_target_pairs={{0,128},{128,0},{1,129},{129,1},{2,130},{130,2},{3,131},{131,3},{4... | collective-permute-start | bytes 4128776 | tf_op jit(solution)/shard_map/ppermute | solution.py:30
  60.9 1.0 copy-start
  61.9 17.5 %copy-start.4 = (f32[768]{0:T(1024)S(1)}, f32[768]{0:T(1024)}, u32[]{:S(2)}) copy-start(f32[768]{0:T(1024)} %bias.1) | copy-start | bytes 9220
  61.9 17.5 %all-to-all-start.1 = ((bf16[4,128,1152]{2,1,0:T(8,128)(2,1)}), bf16[4,128,1152]{2,1,0:T(8,128)(2,1)}, u32[]{:S(2)}, u32[]{:S(2)}) async-start(bf16[4,128,1152]{2,1,0:T(8,128)(2,1)} %copy-done), calls=%async_computation.1 | async-start | bytes 2359296 | tf_op jit(solution)/shard_map/all_to_all | solution.py:34
  96.4 2.5 %collective-permute-start.5 = (bf16[4,64,768]{2,1,0:T(8,128)(2,1)S(1)}, bf16[4,64,768]{2,1,0:T(8,128)(2,1)S(1)}, u32[]{:S(2)}, u32[]{:S(2)}) collective-permute-start(bf16[4,64,768]{2,1,0:T(8,128)(2,1)S(1)} %output_sent.2), channel_id=1, source_target_pairs={{0,1},{1,0},{2,3},{3,2},{4,5},{5,4},{6,7},{7,6},{8,9},{9,8},{10,11... | collective-permute-start | bytes 1179656 | tf_op jit(solution)/shard_map/ppermute | solution.py:30
  97.2 1.9 %collective-permute-start.6 = (bf16[4,64,768]{2,1,0:T(8,128)(2,1)S(1)}, bf16[4,64,768]{2,1,0:T(8,128)(2,1)S(1)}, u32[]{:S(2)}, u32[]{:S(2)}) collective-permute-start(bf16[4,64,768]{2,1,0:T(8,128)(2,1)S(1)} %output_sent.3), channel_id=1, source_target_pairs={{0,1},{1,0},{2,3},{3,2},{4,5},{5,4},{6,7},{7,6},{8,9},{9,8},{10,11... | collective-permute-start | bytes 1179656 | tf_op jit(solution)/shard_map/ppermute | solution.py:30
  99.3 34.7 %copy-start.2 = (bf16[4,6144]{1,0:T(4,128)(2,1)S(1)}, bf16[4,6144]{1,0:T(4,128)(2,1)}, u32[]{:S(2)}) copy-start(bf16[4,6144]{1,0:T(4,128)(2,1)} %tokens.3) | copy-start | bytes 147460
